TPU v7x, 768 devices: a whole 4x8x12 slice. The times are simulated.
768 devices in a mesh: rep: 48 (over y_lo, z, core), fsdp: 16 (over x, y_hi).
Axes of the slice: x: 4, y: 8 (y_hi: 4, y_lo: 2; y = y_hi * 2 + y_lo), z: 12, core: 2. Of those that a mesh axis runs over, the one named last changes fastest.
Arguments:
- tokens: bfloat16 [48, 2048, 8192], P('rep', 'fsdp'), may hold values from -6 to 6
- norm_gain: bfloat16 [8192], replicated, may hold values from 0.25 to 1.75
- inner_weight: bfloat16 [48, 8192, 512], P('rep', 'fsdp'), may hold values from -0.0625 to 0.0625
- cotangent: bfloat16 [48, 2048, 512], P('rep', 'fsdp'), may hold values from -6 to 6
- fragment: bfloat16 [48, 8192, 512], P('rep', 'fsdp'), may hold values from -6 to 6
- outer_param: float32 [8192, 512], P('fsdp'), may hold values from -6 to 6
- momentum: bfloat16 [8192, 512], P('fsdp'), may hold values from -3 to 3
- lag: int32 [48], P('rep'), may hold values from 0 to 7, as said below
- threshold: int32 [1], replicated, may hold values from 1 to 6
Outputs:
- inner_grad: bfloat16 [48, 8192, 512], P('rep', 'fsdp')
- mixed: bfloat16 [48, 8192, 512], P('rep', 'fsdp')
- new_momentum: bfloat16 [8192, 512], P('fsdp')
Inputs may be any that keep to these rules, and one draw needn't show every extreme that they name: At least one replica has lag 0.
All inputs are finite; a program needn't handle non-finite values.
Results may differ from a plain program's by a relative error of at most 0.006.
Values may be sent and summed in bfloat16 or wider, within the bound.
A program may use at most 64 MiB of HBM per device.

v0:
```python
import math

import jax
import jax.numpy as jnp
from jax import lax
from jax.sharding import PartitionSpec as P

EPS = 1e-05
MU = 0.9
OUTER_LR = 0.7
ALPHA = 0.5


def laid_out(blocks, dim):
    shape = list(blocks.shape[1:])
    shape[dim] *= blocks.shape[0]
    return jnp.moveaxis(blocks, 0, dim).reshape(shape)


def copy_for_each(value, axis):
    copies = jnp.broadcast_to(value, (lax.axis_size(axis), *value.shape))
    return lax.all_to_all(copies, axis, split_axis=0, concat_axis=0, tiled=True)


def gather_directly(value, axis, dim):
    return laid_out(copy_for_each(value, axis), dim)


def taken_together(value, axis):
    return copy_for_each(value, axis).sum(axis=0)


def split_up(value, dim, length):
    shape = value.shape
    blocks = value.reshape(*shape[:dim], length, shape[dim] // length, *shape[dim + 1 :])
    return jnp.moveaxis(blocks, dim, 0)


def sum_at_owner(value, axis, dim):
    blocks = split_up(value, dim, lax.axis_size(axis))
    arrived = lax.all_to_all(blocks, axis, split_axis=0, concat_axis=0, tiled=True)
    return arrived.sum(axis=0)


def in_one_piece(arrays, axis, dim, along):
    both = jnp.concatenate(arrays, axis=along)
    out, at, gathered = (lax.all_gather(both, axis, axis=dim, tiled=True), 0, [])
    for a in arrays:
        gathered.append(lax.slice_in_dim(out, at, at + a.shape[along], axis=along))
        at += a.shape[along]
    return tuple(gathered)


def inner_part(tokens, norm_gain, inner_weight, cotangent):
    values = tokens[0].astype(jnp.float32)
    normed = (
        values
        * lax.rsqrt(jnp.mean(values * values, axis=1, keepdims=True) + EPS)
        * norm_gain.astype(jnp.float32)
    ).astype(jnp.bfloat16)
    key_rows = jnp.dot(
        normed,
        lax.all_gather(inner_weight[0], "fsdp", axis=0, tiled=True),
        preferred_element_type=jnp.float32,
    )
    sigmoid_keys = jax.nn.sigmoid(key_rows)
    dkeys = (
        cotangent[0].astype(jnp.float32) * sigmoid_keys * (1.0 + key_rows * (1.0 - sigmoid_keys))
    ).astype(jnp.bfloat16)
    feature_block = lax.all_to_all(normed, "fsdp", split_axis=1, concat_axis=0, tiled=True)
    gradient = lax.dot_general(
        feature_block,
        gather_directly(dkeys, "fsdp", 0),
        (((0,), (0,)), ((), ())),
        preferred_element_type=jnp.float32,
    )
    total_tokens = normed.shape[0] * lax.axis_size("fsdp")
    return (gradient * (1.0 / math.sqrt(total_tokens)))[None].astype(jnp.bfloat16)


def fragment_part(fragment, outer_param, momentum, lag, threshold):
    local_frag = fragment[0].astype(jnp.float32)
    flag = (lag[0] <= threshold[0]).astype(jnp.float32)
    count = taken_together(flag, "rep")
    scale = 1.0 / count
    pseudo_grad = flag * (outer_param - local_frag)
    flat_size = outer_param.shape[0] * outer_param.shape[1]
    replicas = lax.axis_size("rep")
    share_len = -(-flat_size // (replicas * 128)) * 128
    padded_len = replicas * share_len

    def spread(array):
        return jnp.pad(array.reshape(-1), (0, padded_len - flat_size)).reshape(
            padded_len // 128, 128
        )

    share = sum_at_owner(spread(pseudo_grad), "rep", 0)
    offset = lax.axis_index("rep") * (share_len // 128)
    outer_slice = lax.dynamic_slice_in_dim(spread(outer_param), offset, share_len // 128, 0)
    moment_slice = lax.dynamic_slice_in_dim(
        spread(momentum.astype(jnp.float32)), offset, share_len // 128, 0
    )
    average = share * scale
    moment_new = MU * moment_slice + average
    outer_new = outer_slice - OUTER_LR * (average + MU * moment_new)
    gathered = in_one_piece((outer_new, moment_new), "rep", 0, 1)
    new_outer = gathered[0].reshape(-1)[:flat_size].reshape(outer_param.shape)
    moment = gathered[1].reshape(-1)[:flat_size].reshape(outer_param.shape)
    mixed = (ALPHA * local_frag + (1.0 - ALPHA) * new_outer)[None].astype(jnp.bfloat16)
    return (mixed, moment.astype(jnp.bfloat16))


def shards(
    tokens, norm_gain, inner_weight, cotangent, fragment, outer_param, momentum, lag, threshold
):
    inner_grad = inner_part(tokens, norm_gain, inner_weight, cotangent)
    mixed, new_momentum = fragment_part(fragment, outer_param, momentum, lag, threshold)
    return (inner_grad, mixed, new_momentum)


def solution(mesh):
    placed = (
        P("rep", "fsdp", None),
        P(),
        P("rep", "fsdp", None),
        P("rep", "fsdp", None),
        P("rep", "fsdp", None),
        P("fsdp", None),
        P("fsdp", None),
        P("rep"),
        P(),
    )
    return jax.shard_map(
        shards,
        mesh=mesh,
        in_specs=placed,
        out_specs=(P("rep", "fsdp", None), P("rep", "fsdp", None), P("fsdp", None)),
        check_vma=False,
    )
```

profile of v0, /device:TPU:6, one launch (start us, length us, event | category | flops | bytes accessed | tf_op | source)
XLA Modules:
  0.0 321.3 jit_solution(3260776510560705196)
XLA Ops:
  7.2 0.7 all-gather.5.cloned.1.call-update
  9.2 0.6 broadcast_in_dim.5
  9.8 16.8 %all-to-all-start.3 = ((f32[48,1,1]{2,1,0:T(1,128)}), f32[48,1,1]{2,1,0:T(1,128)S(1)}, u32[]{:S(2)}, u32[]{:S(2)}) async-start(f32[48,1,1]{2,1,0:T(1,128)} %broadcast_in_dim.5), calls=%async_computation.3 | async-start | bytes 49152 | tf_op jit(solution)/shard_map/all_to_all | solution.py:22
  26.7 1.5 fusion.27
  28.2 0.3 copy.20
  28.6 1.1 reshape_reshape.3
  29.7 7.7 %all-to-all-done.3 = f32[48,1,1]{2,1,0:T(1,128)S(1)} async-done(((f32[48,1,1]{2,1,0:T(1,128)}), f32[48,1,1]{2,1,0:T(1,128)S(1)}, u32[]{:S(2)}, u32[]{:S(2)}) %all-to-all-start.3) | async-done | bytes 224 | tf_op jit(solution)/shard_map/all_to_all | solution.py:22
  37.3 4.6 %all-to-all-start.2 = ((f32[48,43,128]{2,1,0:T(8,128)}), f32[48,43,128]{2,1,0:T(8,128)S(1)}, u32[]{:S(2)}, u32[]{:S(2)}) async-start(f32[48,43,128]{2,1,0:T(8,128)} %reshape_reshape.3), calls=%async_computation.2 | async-start | bytes 2359296 | tf_op jit(solution)/shard_map/all_to_all | solution.py:41
  42.0 3.0 copy.16
  45.0 0.5 fusion.2
  45.5 3.9 %multiply_convert_fusion = bf16[128,16,512]{0,2,1:T(8,128)(2,1)} fusion(f32[128,16,512]{0,2,1:T(8,128)} %bitcast.66, f32[16,512]{1,0:T(8,128)S(1)} %mul.80, f32[128]{0:T(128)S(1)} %add_rsqrt_fusion), kind=kLoop, calls=%fused_computation.7 | loop fusion | flops 3145728 | bytes 6324736 | tf_op jit(solution)/shard_map/convert_element_type | solution.py:60
  49.4 33.9 %all-to-all-done.2 = f32[48,43,128]{2,1,0:T(8,128)S(1)} async-done(((f32[48,43,128]{2,1,0:T(8,128)}), f32[48,43,128]{2,1,0:T(8,128)S(1)}, u32[]{:S(2)}, u32[]{:S(2)}) %all-to-all-start.2) | async-done | bytes 1056800 | tf_op jit(solution)/shard_map/all_to_all | solution.py:41
  83.3 9.4 %all-to-all-start = ((bf16[128,16,512]{0,2,1:T(8,128)(2,1)}), bf16[128,16,512]{0,2,1:T(8,128)(2,1)}, u32[]{:S(2)}, u32[]{:S(2)}) async-start(bf16[128,16,512]{0,2,1:T(8,128)(2,1)} %multiply_convert_fusion), calls=%async_computation | async-start | bytes 4194304 | tf_op jit(solution)/shard_map/all_to_all | solution.py:70
  92.7 2.5 copy.19
  95.2 2.0 copy.21
  97.2 1.9 pad_bitcast_fusion.1
  99.2 2.4 pad_bitcast_fusion
  101.5 0.7 reduce_sum.29
  102.9 0.8 multiply_subtract_fusion
  103.7 0.6 maximum_bitcast_fusion
  104.4 93.7 %all-gather.5.cloned.1.call-done = bf16[1,8192,512]{2,1,0:T(8,128)(2,1)} async-done(((bf16[1,512,512]{2,1,0:T(8,128)(2,1)}), bf16[1,8192,512]{2,1,0:T(8,128)(2,1)}) %all-gather.5.cloned.1.call-update) | async-done | bytes 8388624 | tf_op jit(solution)/shard_map/all_gather | solution.py:63
  198.1 4.8 %fusion.29 = bf16[128,512]{1,0:T(8,128)(2,1)S(1)} fusion(bf16[1,8192,512]{2,1,0:T(8,128)(2,1)} %all-gather.5.cloned.1.call-done, bf16[1,128,8192]{2,1,0:T(8,128)(2,1)S(1)} %copy-done, f32[8192]{0:T(1024)S(1)} %convert_element_type.69, f32[128]{0:T(128)S(1)} %add_rsqrt_fusion, bf16[1,128,512]{2,1,0:T(8,128)(2,1)S(1)} %copy-done.4), kind=kOutput, calls=%fused_computation.29 | convolution fusion | flops 1078591488 | bytes 10781184 | tf_op jit(solution)/shard_map/dot_general | solution.py:61
  202.8 1.5 broadcast_in_dim.4
  204.4 6.9 %all-to-all-start.1 = ((bf16[16,128,512]{2,1,0:T(8,128)(2,1)}), bf16[16,128,512]{2,1,0:T(8,128)(2,1)}, u32[]{:S(2)}, u32[]{:S(2)}) async-start(bf16[16,128,512]{2,1,0:T(8,128)(2,1)} %broadcast_in_dim.4), calls=%async_computation.1 | async-start | bytes 4194304 | tf_op jit(solution)/shard_map/all_to_all | solution.py:22
  211.2 93.2 %all-gather.7.cloned.1.call-done = f32[48,43,256]{2,1,0:T(8,128)} async-done(((f32[1,43,256]{2,1,0:T(8,128)}), f32[48,43,256]{2,1,0:T(8,128)}) %all-gather.7.cloned.1.call-update) | async-done | bytes 2113552 | tf_op jit(solution)/shard_map/all_gather | solution.py:47
  304.4 1.8 reshape.92
  306.2 0.9 slice.18
  307.1 0.2 reshape.82
  307.3 0.9 copy-done.1
  308.1 1.1 convert_element_type.83
  309.3 1.0 fusion.24
  310.2 4.3 %fusion.20 = bf16[1,512,512]{2,1,0:T(8,128)(2,1)} fusion(bf16[16,128,512]{2,1,0:T(8,128)(2,1)} %all-to-all-done.1, bf16[128,16,512]{0,2,1:T(8,128)(2,1)} %all-to-all-done), kind=kOutput, calls=%fused_computation.18 | convolution fusion | flops 1074266112 | bytes 4718592 | tf_op jit(solution)/shard_map/dot_general | solution.py:71
  (20 shorter events, 0.4 us)
Async XLA Ops:
  7.2 190.9 %all-gather.5.cloned.1.call-start = ((), (), s32[]{:S(2)}) async-start(), calls=%async_computation.4 | async-start | bytes 8912896 | tf_op jit(solution)/shard_map/all_gather | solution.py:63
  9.8 27.5 %all-to-all-start.3 = ((f32[48,1,1]{2,1,0:T(1,128)}), f32[48,1,1]{2,1,0:T(1,128)S(1)}, u32[]{:S(2)}, u32[]{:S(2)}) async-start(f32[48,1,1]{2,1,0:T(1,128)} %broadcast_in_dim.5), calls=%async_computation.3 | async-start | bytes 49152 | tf_op jit(solution)/shard_map/all_to_all | solution.py:22
  28.6 13.4 %copy-start = (bf16[1,128,8192]{2,1,0:T(8,128)(2,1)S(1)}, bf16[1,128,8192]{2,1,0:T(8,128)(2,1)}, u32[]{:S(2)}) copy-start(bf16[1,128,8192]{2,1,0:T(8,128)(2,1)} %param.9) | copy-start | bytes 6291460
  37.3 46.0 %all-to-all-start.2 = ((f32[48,43,128]{2,1,0:T(8,128)}), f32[48,43,128]{2,1,0:T(8,128)S(1)}, u32[]{:S(2)}, u32[]{:S(2)}) async-start(f32[48,43,128]{2,1,0:T(8,128)} %reshape_reshape.3), calls=%async_computation.2 | async-start | bytes 2359296 | tf_op jit(solution)/shard_map/all_to_all | solution.py:41
  41.9 3.0 copy-start.3
  83.3 119.5 %all-to-all-start = ((bf16[128,16,512]{0,2,1:T(8,128)(2,1)}), bf16[128,16,512]{0,2,1:T(8,128)(2,1)}, u32[]{:S(2)}, u32[]{:S(2)}) async-start(bf16[128,16,512]{0,2,1:T(8,128)(2,1)} %multiply_convert_fusion), calls=%async_computation | async-start | bytes 4194304 | tf_op jit(solution)/shard_map/all_to_all | solution.py:70
  92.7 211.7 %all-gather.7.cloned.1.call-start = ((), (), s32[]{:S(2)}) async-start(), calls=%async_computation.5 | async-start | bytes 2408448 | tf_op jit(solution)/shard_map/all_gather | solution.py:47
  97.2 100.8 %copy-start.4 = (bf16[1,128,512]{2,1,0:T(8,128)(2,1)S(1)}, bf16[1,128,512]{2,1,0:T(8,128)(2,1)}, u32[]{:S(2)}) copy-start(bf16[1,128,512]{2,1,0:T(8,128)(2,1)} %param.12) | copy-start | bytes 393220
  204.4 105.9 %all-to-all-start.1 = ((bf16[16,128,512]{2,1,0:T(8,128)(2,1)}), bf16[16,128,512]{2,1,0:T(8,128)(2,1)}, u32[]{:S(2)}, u32[]{:S(2)}) async-start(bf16[16,128,512]{2,1,0:T(8,128)(2,1)} %broadcast_in_dim.4), calls=%async_computation.1 | async-start | bytes 4194304 | tf_op jit(solution)/shard_map/all_to_all | solution.py:22
  307.1 1.0 copy-start.1
  307.1 2.1 copy-start.2
Sparse Core Ops, SparseCore 0:
  11.6 186.4 all-gather.4
  201.1 103.2 all-gather.6
where the time goes:
time: 323 us; the launch traced here: 321 us
  waiting for transfers between devices  229 us (71%)
  starting transfers between devices  37.7 us (12%)
  local copies, waits for them, and re-layouts  20.3 us (6%)
  between operations  16.2 us (5%)
  other arithmetic  9.03 us (3%)
  matrix products  9.03 us (3%)
    all_gather x1, waiting for transfers between devices, inner_part(): lax.all_gather(inner_weight[0], 'fsdp', axis=0, tiled=True)  93.7 us
    all_gather x1, waiting for transfers between devices, in_one_piece(): lax.all_gather(both, axis, axis=dim, tiled=True)  93.2 us
    all_to_all x1, waiting for transfers between devices, sum_at_owner(): lax.all_to_all(blocks, axis, split_axis=0, concat_axis=0, tiled=True)  33.9 us
    all_to_all x2, starting transfers between devices, copy_for_each(): return lax.all_to_all(copies, axis, split_axis=0, concat_axis=0, tiled=True)  23.7 us
    all_to_all x1, starting transfers between devices, inner_part(): lax.all_to_all(normed, 'fsdp', split_axis=1, concat_axis=0, tiled=True)  9.37 us
    unnamed x15, local copies, waits for them, and re-layouts  9.35 us
    all_to_all x2, waiting for transfers between devices, copy_for_each(): return lax.all_to_all(copies, axis, split_axis=0, concat_axis=0, tiled=True)  7.67 us
  transfers between devices with their start and end apart: 6, of which 4 were waited for; matrix products, arithmetic and copies ran while one was open for 10% of the time, Pallas kernels for 0%

commit v1 on v0

v1 whole, which is shorter than its diff:
```python
import math

import jax
import jax.numpy as jnp
from jax import lax
from jax.experimental import pallas as pl
from jax.experimental.pallas import tpu as pltpu
from jax.sharding import PartitionSpec as P

EPS = 1e-05
MU = 0.9
OUTER_LR = 0.7
ALPHA = 0.5

NX, NY, NZ = 4, 4, 12
TOK = 128
FB = 512
KV = 512
NK = 4
KC = KV // NK
SHARE = 96
PACK = SHARE + 16
HALF = 1024
F32, BF16 = jnp.float32, jnp.bfloat16
MESH = pl.DeviceIdType.MESH


def kernel(
    tokens, gain, weight, cotangent, fragment, outer, momentum, lag, threshold,
    grad_out, mixed_out, mom_out,
    tokv, tokr, rst_s, rst_r, nrm, nrt, wown, wq, cotv,
    rs_own, rs_s, rs_r, ry_s, ry_r, dk, g_own, g_s, g_r, gout,
    fragv, outv, momv, msk, f1r, zs, zr, ys, yr, avg, mixv, momo,
    local_sem, tok_ss, tok_rs, rst_ss, rst_rs, w_ss, w_rs,
    rx_ss, rx_rs, ry_ss, ry_rs, ay_ss, ay_rs, ax_ss, ax_rs, gr_ss, gr_rs,
    f_ss, f_rs, z_ss, z_rs, az_ss, az_rs, out_sem,
):
    rep, fs = lax.axis_index("rep"), lax.axis_index("fsdp")
    core, z, ylo = lax.rem(rep, 2), lax.rem(rep // 2, NZ), rep // (2 * NZ)
    x, y = fs // NY, lax.rem(fs, NY)
    s = 1 - 2 * lax.rem(y + core, 2)
    yp = lax.rem(y + s + NY, NY)
    yq = lax.rem(y - s + NY, NY)
    yo = lax.rem(y + 2, NY)

    def at(i, yy):
        return (rep, lax.rem(x + i + NX, NX) * NY + yy)

    def at_z(i):
        return (ylo * 2 * NZ + lax.rem(z + i, NZ) * 2 + core, fs)

    other_core = (ylo * 2 * NZ + z * 2 + (1 - core), fs)
    other_ylo = ((1 - ylo) * 2 * NZ + z * 2 + core, fs)
    group = [(i, e) for e in (1, 0) for i in (2, 1, 3, 0) if (i, e) != (0, 0)]

    def remote(src, dst, ss, rs, device):
        return pltpu.make_async_remote_copy(
            src_ref=src, dst_ref=dst, send_sem=ss, recv_sem=rs, device_id=device, device_id_type=MESH
        )

    barrier = pltpu.get_barrier_semaphore()
    peers = [at(i, yp if e else y) for i, e in group] + [at(0, yq), other_core, other_ylo]
    peers += [at_z(i) for i in range(1, NZ)]
    for peer in peers:
        pl.semaphore_signal(barrier, inc=1, device_id=peer, device_id_type=MESH)

    tok_in = [
        pltpu.make_async_copy(tokens.at[0, :, pl.ds(b * FB, FB)], tokv.at[b], local_sem.at[b])
        for b in range(NX * NY)
    ]
    w_in = [
        pltpu.make_async_copy(weight.at[0, :, pl.ds(k * KC, KC)], wown.at[k], local_sem.at[16 + k])
        for k in range(NK)
    ]
    frag_in = [
        pltpu.make_async_copy(fragment.at[0, :, pl.ds(c * 128, 128)], fragv.at[c], local_sem.at[20 + c])
        for c in range(4)
    ]
    out_in = [
        pltpu.make_async_copy(outer.at[:, pl.ds(c * 128, 128)], outv.at[c], local_sem.at[24 + c])
        for c in range(4)
    ]
    mom_in = [
        pltpu.make_async_copy(momentum.at[:, pl.ds(c * 128, 128)], momv.at[c], local_sem.at[28 + c])
        for c in range(4)
    ]
    cot_in = pltpu.make_async_copy(cotangent.at[0], cotv, local_sem.at[32])
    loads = tok_in + w_in + frag_in + out_in + [cot_in] + mom_in
    for copy in loads:
        copy.start()
    for copy in tok_in + w_in:
        copy.wait()
    pl.semaphore_wait(barrier, len(peers))

    tok_copies = {}
    for n, (i, e) in enumerate(group):
        yd = yp if e else y
        cross = yo if e else yq
        xd = lax.rem(x + i, NX)
        for f, yf in enumerate((yd, cross)):
            copy = remote(
                tokv.at[xd * NY + yf], tokr.at[f, i * 2 + e],
                tok_ss.at[2 * n + f], tok_rs.at[2 * n + f], at(i, yd),
            )
            copy.start()
            tok_copies[i, e, f] = copy
    w_copies = [
        remote(wown.at[k], wq.at[k], w_ss.at[k], w_rs.at[k], at(0, yq)) for k in range(NK)
    ]
    for copy in w_copies:
        copy.start()

    flag = jnp.where(lag[0] <= threshold[0], 1.0, 0.0).astype(F32)
    for copy in frag_in:
        copy.wait()
    for h in range(2):
        part = fragv[(1 - core) * 2 + h].astype(F32) * flag
        msk[pl.ds(h * 512, 512), :] = part.astype(BF16)
    msk[pl.ds(HALF, 16), :] = jnp.full((16, 128), flag, F32).astype(BF16)
    f1_copy = remote(msk, f1r, f_ss.at[0], f_rs.at[0], other_core)
    f1_copy.start()

    def square(b, total):
        v = tokv[b].astype(F32)
        v = v * v
        return total + (v[:, 0:128] + v[:, 128:256]) + (v[:, 256:384] + v[:, 384:512])

    sums = lax.fori_loop(0, NX * NY, square, jnp.zeros((TOK, 128), F32))
    scale_own = lax.rsqrt(jnp.sum(sums, axis=1, keepdims=True) * (1.0 / (NX * NY * FB)) + EPS)
    rst_s[...] = jnp.broadcast_to(scale_own, (TOK, 128)).T[0:8, :]
    rst_copies = {}
    for n, (i, e) in enumerate(group):
        copy = remote(
            rst_s, rst_r.at[i * 2 + e], rst_ss.at[n], rst_rs.at[n], at(i, yp if e else y)
        )
        copy.start()
        rst_copies[i, e] = copy

    gains = [gain[pl.ds(x * NY + yy, 1), :] for yy in (y, yq)]

    def normalise(i, e):
        slot = i * 2 + e
        if slot == 0:
            scale = scale_own
        else:
            rst_copies[i, e].wait_recv()
            scale = jnp.broadcast_to(rst_r[slot, 0:1, :], (TOK, 128)).T[:, 0:1]
        for f in range(2):
            if slot == 0:
                raw = tokv[x * NY + (yq if f else y)]
            else:
                tok_copies[i, e, f].wait_recv()
                raw = tokr[f, slot]
            v = raw.astype(F32) * scale * gains[f]
            nrm[f, pl.ds(slot * TOK, TOK), :] = v.astype(BF16)
            nrt[f, :, pl.ds(slot * TOK, TOK)] = v.T.astype(BF16)

    normalise(0, 0)

    f1_copy.wait_recv()
    for copy in out_in:
        copy.wait()
    both = f1r[pl.ds(HALF, 16), :].astype(F32) + flag
    row = both[0:1, :]
    for j in range(NZ):
        for r in range(0, SHARE, 32):
            first = j * SHARE + r
            if first < HALF:
                block, at_row = core * 2 + first // 512, first % 512
                mine = fragv[block, pl.ds(at_row, 32), :].astype(F32) * flag
                theirs = f1r[pl.ds(first, 32), :].astype(F32)
                value = row * outv[block, pl.ds(at_row, 32), :] - (mine + theirs)
            else:
                value = jnp.zeros((32, 128), F32)
            zs[j, pl.ds(r, 32), :] = value.astype(BF16)
        zs[j, pl.ds(SHARE, 16), :] = both.astype(BF16)
    z_copies = [
        remote(zs.at[lax.rem(z + i, NZ)], zr.at[i], z_ss.at[i], z_rs.at[i], at_z(i))
        for i in (6, 5, 7, 4, 8, 3, 9, 2, 10, 1, 11)
    ]
    for copy in z_copies:
        copy.start()

    for i, e in ((1, 0), (3, 0), (2, 0), (0, 1), (1, 1), (3, 1), (2, 1)):
        normalise(i, e)

    rx, ry, ay, ax, gr = {}, {}, {}, {}, {}

    def keys_partial(k):
        w_copies[k].wait_recv()
        for i in (2, 1, 3, 0):
            rows = pl.ds(i * 2 * TOK, 2 * TOK)
            part = jnp.dot(nrm[0, rows, :], wown[k], preferred_element_type=F32)
            part += jnp.dot(nrm[1, rows, :], wq[k], preferred_element_type=F32)
            if i == 0:
                rs_own[k] = part
            else:
                rs_s[k, i] = part.astype(BF16)
                n = k * NX + i
                rx[k, i] = remote(rs_s.at[k, i], rs_r.at[k, i], rx_ss.at[n], rx_rs.at[n], at(-i, y))
                rx[k, i].start()

    def sum_x(k):
        for i in (1, 3, 2):
            rx[k, i].wait_recv()
        total = rs_own[k]
        for i in (1, 2, 3):
            total += rs_r[k, i].astype(F32)
        rs_own[k] = total
        ry_s[k] = total[TOK:, :].astype(BF16)
        ry[k] = remote(ry_s.at[k], ry_r.at[k], ry_ss.at[k], ry_rs.at[k], at(0, yp))
        ry[k].start()

    def send_x(k, e):
        for i in (2, 1, 3):
            n = (k * NX + i) * 2 + e
            ax[k, i, e] = remote(
                dk.at[k, pl.ds(e * TOK, TOK)], dk.at[k, pl.ds((i * 2 + e) * TOK, TOK)],
                ax_ss.at[n], ax_rs.at[n], at(i, y),
            )
            ax[k, i, e].start()

    def dkeys(k):
        ry[k].wait_recv()
        keys = rs_own[k, 0:TOK, :] + ry_r[k].astype(F32)
        sig = jax.nn.sigmoid(keys)
        cot = cotv[:, pl.ds(k * KC, KC)].astype(F32)
        dk[k, 0:TOK, :] = (cot * sig * (1.0 + keys * (1.0 - sig))).astype(BF16)
        ay[k] = remote(
            dk.at[k, pl.ds(0, TOK)], dk.at[k, pl.ds(TOK, TOK)], ay_ss.at[k], ay_rs.at[k], at(0, yp)
        )
        ay[k].start()
        send_x(k, 0)

    def forward(k):
        ay[k].wait_recv()
        send_x(k, 1)

    def gradient(k):
        for e in range(2):
            for i in (1, 3, 2):
                ax[k, i, e].wait_recv()
        g_s[k] = jnp.dot(nrt[1], dk[k], preferred_element_type=F32).astype(BF16)
        gr[k] = remote(g_s.at[k], g_r.at[k], gr_ss.at[k], gr_rs.at[k], at(0, yq))
        gr[k].start()
        g_own[k] = jnp.dot(nrt[0], dk[k], preferred_element_type=F32)

    outs = []

    def finish(k):
        gr[k].wait_recv()
        total = g_own[k] + g_r[k].astype(F32)
        gout[k] = (total * (1.0 / math.sqrt(NX * NY * TOK))).astype(BF16)
        copy = pltpu.make_async_copy(gout.at[k], grad_out.at[0, :, pl.ds(k * KC, KC)], out_sem.at[k])
        copy.start()
        outs.append(copy)

    y_copy = remote(ys, yr, f_ss.at[1], f_rs.at[1], other_ylo)

    def sum_z():
        total = zs[z].astype(F32)
        for copy in z_copies:
            copy.wait_recv()
        for i in range(1, NZ):
            total += zr[i].astype(F32)
        ys[...] = total
        y_copy.start()

    own_share = avg.at[core, pl.ds(pl.multiple_of(z * SHARE, SHARE), SHARE)]
    az_copies = [
        remote(own_share, own_share, az_ss.at[i], az_rs.at[i], at_z(i))
        for i in (6, 5, 7, 4, 8, 3, 9, 2, 10, 1, 11)
    ]
    core_copy = remote(avg.at[core], avg.at[core], f_ss.at[2], f_rs.at[2], other_core)

    def share_average():
        y_copy.wait_recv()
        total = ys[...] + yr[...]
        scale = 1.0 / total[SHARE : SHARE + 1, :]
        own_share[...] = (total[0:SHARE, :] * scale).astype(BF16)
        for copy in az_copies:
            copy.start()

    def gather_average():
        for copy in az_copies:
            copy.wait_recv()
        core_copy.start()

    def outer_update():
        for copy in mom_in:
            copy.wait()
        core_copy.wait_recv()
        for c in range(4):
            average = avg[c // 2, pl.ds(c % 2 * 512, 512), :].astype(F32)
            moment = MU * momv[c].astype(F32) + average
            new_outer = outv[c] - OUTER_LR * (average + MU * moment)
            mixv[c] = (ALPHA * fragv[c].astype(F32) + (1.0 - ALPHA) * new_outer).astype(BF16)
            momo[c] = moment.astype(BF16)
            for buf, out, n in ((mixv, mixed_out.at[0], 4 + c), (momo, mom_out, 8 + c)):
                copy = pltpu.make_async_copy(buf.at[c], out.at[:, pl.ds(c * 128, 128)], out_sem.at[n])
                copy.start()
                outs.append(copy)

    cot_in.wait()
    stages = [keys_partial, sum_x, dkeys, forward, gradient, finish]
    extra = {1: sum_z, 2: share_average, 5: gather_average, 6: outer_update}
    for slot in range(NK + len(stages) - 1):
        for n in reversed(range(len(stages))):
            if 0 <= slot - n < NK:
                stages[n](slot - n)
        if slot in extra:
            extra[slot]()

    for copy in outs:
        copy.wait()
    sent = list(tok_copies.values()) + w_copies + [f1_copy, y_copy, core_copy]
    sent += list(rst_copies.values()) + z_copies + az_copies
    for group_of in (rx, ry, ay, ax, gr):
        sent += list(group_of.values())
    for copy in sent:
        copy.wait_send()


def shards(
    tokens, norm_gain, inner_weight, cotangent, fragment, outer_param, momentum, lag, threshold
):
    vmem, dma = pltpu.VMEM, pltpu.SemaphoreType.DMA
    hbm = pl.BlockSpec(memory_space=pl.ANY)
    smem = pl.BlockSpec(memory_space=pltpu.SMEM)
    return pl.pallas_call(
        kernel,
        out_shape=(
            jax.ShapeDtypeStruct((1, FB, KV), BF16),
            jax.ShapeDtypeStruct((1, FB, KV), BF16),
            jax.ShapeDtypeStruct((FB, KV), BF16),
        ),
        in_specs=[hbm, pl.BlockSpec(memory_space=pltpu.VMEM), hbm, hbm, hbm, hbm, hbm, smem, smem],
        out_specs=(hbm, hbm, hbm),
        scratch_shapes=[
            vmem((16, TOK, FB), BF16),
            vmem((2, 8, TOK, FB), BF16),
            vmem((8, 128), F32),
            vmem((8, 8, 128), F32),
            vmem((2, 8 * TOK, FB), BF16),
            vmem((2, FB, 8 * TOK), BF16),
            vmem((NK, FB, KC), BF16),
            vmem((NK, FB, KC), BF16),
            vmem((TOK, KV), BF16),
            vmem((NK, 2 * TOK, KC), F32),
            vmem((NK, NX, 2 * TOK, KC), BF16),
            vmem((NK, NX, 2 * TOK, KC), BF16),
            vmem((NK, TOK, KC), BF16),
            vmem((NK, TOK, KC), BF16),
            vmem((NK, 8 * TOK, KC), BF16),
            vmem((NK, FB, KC), F32),
            vmem((NK, FB, KC), BF16),
            vmem((NK, FB, KC), BF16),
            vmem((NK, FB, KC), BF16),
            vmem((4, 512, 128), BF16),
            vmem((4, 512, 128), F32),
            vmem((4, 512, 128), BF16),
            vmem((HALF + 16, 128), BF16),
            vmem((HALF + 16, 128), BF16),
            vmem((NZ, PACK, 128), BF16),
            vmem((NZ, PACK, 128), BF16),
            vmem((PACK, 128), F32),
            vmem((PACK, 128), F32),
            vmem((2, NZ * SHARE, 128), BF16),
            vmem((4, 512, 128), BF16),
            vmem((4, 512, 128), BF16),
            dma((33,)),
            dma((14,)), dma((14,)),
            dma((7,)), dma((7,)),
            dma((NK,)), dma((NK,)),
            dma((NK * NX,)), dma((NK * NX,)),
            dma((NK,)), dma((NK,)),
            dma((NK,)), dma((NK,)),
            dma((NK * NX * 2,)), dma((NK * NX * 2,)),
            dma((NK,)), dma((NK,)),
            dma((3,)), dma((3,)),
            dma((NZ,)), dma((NZ,)),
            dma((NZ,)), dma((NZ,)),
            dma((12,)),
        ],
        compiler_params=pltpu.CompilerParams(
            collective_id=0, has_side_effects=True, vmem_limit_bytes=48 * 1024 * 1024
        ),
        name="window",
    )(
        tokens,
        norm_gain.reshape(16, FB).astype(F32),
        inner_weight,
        cotangent,
        fragment,
        outer_param,
        momentum,
        lag,
        threshold,
    )


def solution(mesh):
    placed = (
        P("rep", "fsdp", None),
        P(),
        P("rep", "fsdp", None),
        P("rep", "fsdp", None),
        P("rep", "fsdp", None),
        P("fsdp", None),
        P("fsdp", None),
        P("rep"),
        P(),
    )
    return jax.shard_map(
        shards,
        mesh=mesh,
        in_specs=placed,
        out_specs=(P("rep", "fsdp", None), P("rep", "fsdp", None), P("fsdp", None)),
        check_vma=False,
    )
```

time: 323 us -> 115 us (0.36)
  waiting for transfers between devices: 229 us -> 0 us
  Pallas kernels: 0 us -> 105 us
  starting transfers between devices: 37.7 us -> 0 us
  between operations: 16.2 us -> 1.95 us
  local copies, waits for them, and re-layouts: 20.3 us -> 8.37 us
  matrix products: 9.03 us -> 0 us
  other arithmetic: 9.03 us -> 0 us
    all_gather x2 -> x0, waiting for transfers between devices: 187 us -> none  [the longest x1 93.7 us: inner_part(): lax.all_gather(inner_weight[0], 'fsdp', axis=0, tiled=True)]
    pallas_call x0 -> x1, Pallas kernels: none -> 105 us  [shards(): pl.pallas_call(kernel, out_shape=(jax.ShapeDtypeStruct((1, FB, KV), BF16)...]
    all_to_all x4 -> x0, waiting for transfers between devices: 41.6 us -> none  [the longest x1 33.9 us: sum_at_owner(): lax.all_to_all(blocks, axis, split_axis=0, concat_axis=0, tiled=True)]
    all_to_all x4 -> x0, starting transfers between devices: 37.7 us -> none  [the longest x2 23.7 us: copy_for_each(): return lax.all_to_all(copies, axis, split_axis=0, concat_axis=0, tiled=True)]
    dot_general x2 -> x0, matrix products: 9.03 us -> none  [the longest x1 4.77 us: inner_part(): jnp.dot(normed, lax.all_gather(inner_weight[0], 'fsdp', axis=0, tiled=Tru...]
    convert_element_type x3 -> x0, other arithmetic: 4.86 us -> none  [the longest x1 3.89 us: inner_part(): normed = (values * lax.rsqrt(jnp.mean(values * values, axis=1, keepdims=T...]
    convert_element_type x2 -> x1, local copies, waits for them, and re-layouts: 4.11 us -> 0.74 us  [shards(): norm_gain.reshape(16, FB).astype(F32)]
    unnamed x15 -> x13, local copies, waits for them, and re-layouts: 9.35 us -> 7.63 us
  transfers between devices with their start and end apart: 6 -> 0, of which waited for: 4 -> 0; matrix products, arithmetic and copies ran while one was open for 10% -> 0% of each run, Pallas kernels for 0% -> 0%
where the time goes in v1:
time: 115 us
  Pallas kernels  105 us (91%)
  local copies, waits for them, and re-layouts  8.37 us (7%)
  between operations  1.95 us (2%)
    pallas_call x1, Pallas kernels, shards(): pl.pallas_call(kernel, out_shape=(jax.ShapeDtypeStruct((1, FB, KV), BF16)...  105 us
    unnamed x13, local copies, waits for them, and re-layouts  7.63 us

profile of v1, /device:TPU:6, one launch (start us, length us, event | category | flops | bytes accessed | tf_op | source)
XLA Modules:
  0.0 115.0 jit_solution(8146725130946136391)
XLA Ops:
  1.9 0.7 reshape.9.gain
  2.7 0.0 copy-start
  2.7 1.2 %copy-done = f32[512,512]{1,0:T(8,128)S(1)} copy-done((f32[512,512]{1,0:T(8,128)S(1)}, f32[512,512]{1,0:T(8,128)}, u32[]{:S(2)}) %copy-start) | copy-done | bytes 1048600
  3.9 0.0 copy-start.1
  3.9 1.0 copy-done.1
  4.9 0.0 copy-start.2
  4.9 1.0 copy-done.2
  6.0 0.0 copy-start.3
  6.0 1.0 copy-done.3
  7.0 0.0 copy-start.4
  7.0 0.9 copy-done.4
  7.9 104.7 %window.1 = (bf16[1,512,512]{2,1,0:T(8,128)(2,1)S(1)}, bf16[1,512,512]{2,1,0:T(8,128)(2,1)S(1)}, bf16[512,512]{1,0:T(8,128)(2,1)S(1)}) custom-call(bf16[1,128,8192]{2,1,0:T(8,128)(2,1)} %tokens.1, f32[16,512]{1,0:T(8,128)S(1)} %reshape.9.gain, bf16[1,512,512]{2,1,0:T(8,128)(2,1)S(1)} %copy-done.1, bf16[1,128,512]{2,1,0:T(8,128)(2,1)S(1)} %copy-done.4, ...), custom_call_target="tpu_custom_call" | custom-call | tf_op jit(solution)/shard_map/window/pallas_call | solution.py:330
  112.6 0.8 copy.17
  113.4 0.8 copy.18
  114.2 0.8 copy.19
Async XLA Ops:
  2.7 1.2 %copy-start = (f32[512,512]{1,0:T(8,128)S(1)}, f32[512,512]{1,0:T(8,128)}, u32[]{:S(2)}) copy-start(f32[512,512]{1,0:T(8,128)} %outer.1) | copy-start | bytes 3145732
  3.9 1.0 copy-start.1
  4.9 1.0 copy-start.2
  6.0 1.0 copy-start.3
  7.0 0.9 copy-start.4

commit v2 on v1

--- a/solution.py
+++ b/solution.py
@@ -11,6 +11,8 @@
 MU = 0.9
 OUTER_LR = 0.7
 ALPHA = 0.5
+STARTS = (0.0, 4.3, 8.0, 13.0, 19.0)
+STEP = 2.6
 
 NX, NY, NZ = 4, 4, 12
 TOK = 128
@@ -30,9 +32,9 @@
     grad_out, mixed_out, mom_out,
     tokv, tokr, rst_s, rst_r, nrm, nrt, wown, wq, cotv,
     rs_own, rs_s, rs_r, ry_s, ry_r, dk, g_own, g_s, g_r, gout,
-    fragv, outv, momv, msk, f1r, zs, zr, ys, yr, avg, mixv, momo,
+    gainv, gainf, fragv, outv, momv, msk, f1r, zs, zr, ys, yr, avg, mixv, momo,
     local_sem, tok_ss, tok_rs, rst_ss, rst_rs, w_ss, w_rs,
-    rx_ss, rx_rs, ry_ss, ry_rs, ay_ss, ay_rs, ax_ss, ax_rs, gr_ss, gr_rs,
+    rx_ss, rx_rs, ry_ss, ry_rs, ax_ss, ax_rs, gr_ss, gr_rs,
     f_ss, f_rs, z_ss, z_rs, az_ss, az_rs, out_sem,
 ):
     rep, fs = lax.axis_index("rep"), lax.axis_index("fsdp")
@@ -84,13 +86,16 @@
         pltpu.make_async_copy(momentum.at[:, pl.ds(c * 128, 128)], momv.at[c], local_sem.at[28 + c])
         for c in range(4)
     ]
-    cot_in = pltpu.make_async_copy(cotangent.at[0], cotv, local_sem.at[32])
-    loads = tok_in + w_in + frag_in + out_in + [cot_in] + mom_in
+    cot_in = pltpu.make_async_copy(cotangent.at[0], cotv.at[0], local_sem.at[32])
+    gain_in = pltpu.make_async_copy(gain, gainv, local_sem.at[33])
+    loads = tok_in + w_in + frag_in + out_in + [cot_in, gain_in] + mom_in
     for copy in loads:
         copy.start()
-    for copy in tok_in + w_in:
-        copy.wait()
-    pl.semaphore_wait(barrier, len(peers))
+    with jax.named_scope("load_wait"):
+        for copy in tok_in + w_in:
+            copy.wait()
+    with jax.named_scope("barrier"):
+        pl.semaphore_wait(barrier, len(peers))
 
     tok_copies = {}
     for n, (i, e) in enumerate(group):
@@ -107,8 +112,9 @@
     w_copies = [
         remote(wown.at[k], wq.at[k], w_ss.at[k], w_rs.at[k], at(0, yq)) for k in range(NK)
     ]
-    for copy in w_copies:
-        copy.start()
+    w_copies[0].start()
+    cot_in.wait()
+    cot_copy = remote(cotv.at[0], cotv.at[1], f_ss.at[3], f_rs.at[3], at(0, yp))
 
     flag = jnp.where(lag[0] <= threshold[0], 1.0, 0.0).astype(F32)
     for copy in frag_in:
@@ -136,7 +142,12 @@
         copy.start()
         rst_copies[i, e] = copy
 
-    gains = [gain[pl.ds(x * NY + yy, 1), :] for yy in (y, yq)]
+    gain_in.wait()
+    gainf[...] = gainv[...].astype(F32)
+    gains = [
+        jnp.concatenate([gainf[pl.ds((x * NY + yy) * 4 + j, 1), :] for j in range(4)], axis=1)
+        for yy in (y, yq)
+    ]
 
     def normalise(i, e):
         slot = i * 2 + e
@@ -155,11 +166,13 @@
             nrm[f, pl.ds(slot * TOK, TOK), :] = v.astype(BF16)
             nrt[f, :, pl.ds(slot * TOK, TOK)] = v.T.astype(BF16)
 
-    normalise(0, 0)
-
-    f1_copy.wait_recv()
-    for copy in out_in:
-        copy.wait()
+    with jax.named_scope("norm_own"):
+        normalise(0, 0)
+
+    with jax.named_scope("f1_wait"):
+        f1_copy.wait_recv()
+        for copy in out_in:
+            copy.wait()
     both = f1r[pl.ds(HALF, 16), :].astype(F32) + flag
     row = both[0:1, :]
     for j in range(NZ):
@@ -181,10 +194,45 @@
     for copy in z_copies:
         copy.start()
 
+    y_copy = remote(ys, yr, f_ss.at[1], f_rs.at[1], other_ylo)
+
+    def sum_z():
+        total = zs[z].astype(F32)
+        for copy in z_copies:
+            copy.wait_recv()
+        for i in range(1, NZ):
+            total += zr[i].astype(F32)
+        ys[...] = total
+        y_copy.start()
+
+    own_share = avg.at[core, pl.ds(pl.multiple_of(z * SHARE, SHARE), SHARE)]
+    az_copies = [
+        remote(own_share, own_share, az_ss.at[i], az_rs.at[i], at_z(i))
+        for i in (6, 5, 7, 4, 8, 3, 9, 2, 10, 1, 11)
+    ]
+    core_copy = remote(avg.at[core], avg.at[core], f_ss.at[2], f_rs.at[2], other_core)
+
+    def share_average():
+        y_copy.wait_recv()
+        total = ys[...] + yr[...]
+        scale = 1.0 / total[SHARE : SHARE + 1, :]
+        own_share[...] = (total[0:SHARE, :] * scale).astype(BF16)
+        for copy in az_copies:
+            copy.start()
+
     for i, e in ((1, 0), (3, 0), (2, 0), (0, 1), (1, 1), (3, 1), (2, 1)):
-        normalise(i, e)
-
-    rx, ry, ay, ax, gr = {}, {}, {}, {}, {}
+        with jax.named_scope(f"norm_{i}{e}"):
+            normalise(i, e)
+        if (i, e) == (2, 0):
+            with jax.named_scope("sum_z"):
+                sum_z()
+            w_copies[1].start()
+        if (i, e) == (0, 1):
+            w_copies[2].start()
+            w_copies[3].start()
+            cot_copy.start()
+
+    rx, ry, ax, gr = {}, {}, {}, {}
 
     def keys_partial(k):
         w_copies[k].wait_recv()
@@ -207,39 +255,30 @@
         for i in (1, 2, 3):
             total += rs_r[k, i].astype(F32)
         rs_own[k] = total
-        ry_s[k] = total[TOK:, :].astype(BF16)
+        ry_s[k, 0:TOK, :] = total[TOK:, :].astype(BF16)
+        ry_s[k, TOK:, :] = total[0:TOK, :].astype(BF16)
         ry[k] = remote(ry_s.at[k], ry_r.at[k], ry_ss.at[k], ry_rs.at[k], at(0, yp))
         ry[k].start()
 
-    def send_x(k, e):
+    def dkeys(k):
+        if k == 0:
+            cot_copy.wait_recv()
+        ry[k].wait_recv()
+        keys = rs_own[k] + ry_r[k].astype(F32)
+        sig = jax.nn.sigmoid(keys)
+        cot = cotv[:, :, pl.ds(k * KC, KC)].astype(F32).reshape(2 * TOK, KC)
+        dk[k, 0 : 2 * TOK, :] = (cot * sig * (1.0 + keys * (1.0 - sig))).astype(BF16)
         for i in (2, 1, 3):
-            n = (k * NX + i) * 2 + e
-            ax[k, i, e] = remote(
-                dk.at[k, pl.ds(e * TOK, TOK)], dk.at[k, pl.ds((i * 2 + e) * TOK, TOK)],
+            n = k * NX + i
+            ax[k, i] = remote(
+                dk.at[k, pl.ds(0, 2 * TOK)], dk.at[k, pl.ds(i * 2 * TOK, 2 * TOK)],
                 ax_ss.at[n], ax_rs.at[n], at(i, y),
             )
-            ax[k, i, e].start()
-
-    def dkeys(k):
-        ry[k].wait_recv()
-        keys = rs_own[k, 0:TOK, :] + ry_r[k].astype(F32)
-        sig = jax.nn.sigmoid(keys)
-        cot = cotv[:, pl.ds(k * KC, KC)].astype(F32)
-        dk[k, 0:TOK, :] = (cot * sig * (1.0 + keys * (1.0 - sig))).astype(BF16)
-        ay[k] = remote(
-            dk.at[k, pl.ds(0, TOK)], dk.at[k, pl.ds(TOK, TOK)], ay_ss.at[k], ay_rs.at[k], at(0, yp)
-        )
-        ay[k].start()
-        send_x(k, 0)
-
-    def forward(k):
-        ay[k].wait_recv()
-        send_x(k, 1)
+            ax[k, i].start()
 
     def gradient(k):
-        for e in range(2):
-            for i in (1, 3, 2):
-                ax[k, i, e].wait_recv()
+        for i in (1, 3, 2):
+            ax[k, i].wait_recv()
         g_s[k] = jnp.dot(nrt[1], dk[k], preferred_element_type=F32).astype(BF16)
         gr[k] = remote(g_s.at[k], g_r.at[k], gr_ss.at[k], gr_rs.at[k], at(0, yq))
         gr[k].start()
@@ -254,32 +293,6 @@
         copy = pltpu.make_async_copy(gout.at[k], grad_out.at[0, :, pl.ds(k * KC, KC)], out_sem.at[k])
         copy.start()
         outs.append(copy)
-
-    y_copy = remote(ys, yr, f_ss.at[1], f_rs.at[1], other_ylo)
-
-    def sum_z():
-        total = zs[z].astype(F32)
-        for copy in z_copies:
-            copy.wait_recv()
-        for i in range(1, NZ):
-            total += zr[i].astype(F32)
-        ys[...] = total
-        y_copy.start()
-
-    own_share = avg.at[core, pl.ds(pl.multiple_of(z * SHARE, SHARE), SHARE)]
-    az_copies = [
-        remote(own_share, own_share, az_ss.at[i], az_rs.at[i], at_z(i))
-        for i in (6, 5, 7, 4, 8, 3, 9, 2, 10, 1, 11)
-    ]
-    core_copy = remote(avg.at[core], avg.at[core], f_ss.at[2], f_rs.at[2], other_core)
-
-    def share_average():
-        y_copy.wait_recv()
-        total = ys[...] + yr[...]
-        scale = 1.0 / total[SHARE : SHARE + 1, :]
-        own_share[...] = (total[0:SHARE, :] * scale).astype(BF16)
-        for copy in az_copies:
-            copy.start()
 
     def gather_average():
         for copy in az_copies:
@@ -301,41 +314,58 @@
                 copy.start()
                 outs.append(copy)
 
-    cot_in.wait()
-    stages = [keys_partial, sum_x, dkeys, forward, gradient, finish]
-    extra = {1: sum_z, 2: share_average, 5: gather_average, 6: outer_update}
-    for slot in range(NK + len(stages) - 1):
-        for n in reversed(range(len(stages))):
-            if 0 <= slot - n < NK:
-                stages[n](slot - n)
-        if slot in extra:
-            extra[slot]()
-
-    for copy in outs:
-        copy.wait()
-    sent = list(tok_copies.values()) + w_copies + [f1_copy, y_copy, core_copy]
+    stages = [keys_partial, sum_x, dkeys, gradient, finish]
+    steps = [(t + k * STEP, stage, k) for stage, t in zip(stages, STARTS) for k in range(NK)]
+    outer_stages = ((share_average, 4.0), (gather_average, 20.0), (outer_update, 22.0))
+    steps += [(t, stage, None) for stage, t in outer_stages]
+    for _, stage, k in sorted(steps, key=lambda step: step[0]):
+        with jax.named_scope(f"{stage.__name__}_{k}"):
+            stage() if k is None else stage(k)
+
+    with jax.named_scope("outs"):
+        for copy in outs:
+            copy.wait()
+    sent = list(tok_copies.values()) + w_copies + [f1_copy, y_copy, core_copy, cot_copy]
     sent += list(rst_copies.values()) + z_copies + az_copies
-    for group_of in (rx, ry, ay, ax, gr):
+    for group_of in (rx, ry, ax, gr):
         sent += list(group_of.values())
     for copy in sent:
         copy.wait_send()
+
+
+def put_out(grad, mixed, mom, grad_out, mixed_out, mom_out, g, m, o, sem):
+    into = [pltpu.make_async_copy(a, b, sem.at[n]) for n, (a, b) in enumerate(((grad, g), (mixed, m), (mom, o)))]
+    out = [
+        pltpu.make_async_copy(a, b, sem.at[3 + n])
+        for n, (a, b) in enumerate(((g, grad_out), (m, mixed_out), (o, mom_out)))
+    ]
+    for copy in into:
+        copy.start()
+    for first, second in zip(into, out):
+        first.wait()
+        second.start()
+    for copy in out:
+        copy.wait()
 
 
 def shards(
     tokens, norm_gain, inner_weight, cotangent, fragment, outer_param, momentum, lag, threshold
 ):
     vmem, dma = pltpu.VMEM, pltpu.SemaphoreType.DMA
-    hbm = pl.BlockSpec(memory_space=pl.ANY)
+    hbm = pl.BlockSpec(memory_space=pltpu.HBM)
+    anywhere = pl.BlockSpec(memory_space=pl.ANY)
     smem = pl.BlockSpec(memory_space=pltpu.SMEM)
-    return pl.pallas_call(
+    shapes = (
+        jax.ShapeDtypeStruct((1, FB, KV), BF16),
+        jax.ShapeDtypeStruct((1, FB, KV), BF16),
+        jax.ShapeDtypeStruct((FB, KV), BF16),
+    )
+    results = pl.pallas_call(
         kernel,
-        out_shape=(
-            jax.ShapeDtypeStruct((1, FB, KV), BF16),
-            jax.ShapeDtypeStruct((1, FB, KV), BF16),
-            jax.ShapeDtypeStruct((FB, KV), BF16),
-        ),
-        in_specs=[hbm, pl.BlockSpec(memory_space=pltpu.VMEM), hbm, hbm, hbm, hbm, hbm, smem, smem],
-        out_specs=(hbm, hbm, hbm),
+        out_shape=shapes,
+        in_specs=[hbm] * 7 + [smem, smem],
+
+        out_specs=(anywhere, anywhere, anywhere),
         scratch_shapes=[
             vmem((16, TOK, FB), BF16),
             vmem((2, 8, TOK, FB), BF16),
@@ -345,17 +375,19 @@
             vmem((2, FB, 8 * TOK), BF16),
             vmem((NK, FB, KC), BF16),
             vmem((NK, FB, KC), BF16),
-            vmem((TOK, KV), BF16),
+            vmem((2, TOK, KV), BF16),
             vmem((NK, 2 * TOK, KC), F32),
             vmem((NK, NX, 2 * TOK, KC), BF16),
             vmem((NK, NX, 2 * TOK, KC), BF16),
-            vmem((NK, TOK, KC), BF16),
-            vmem((NK, TOK, KC), BF16),
+            vmem((NK, 2 * TOK, KC), BF16),
+            vmem((NK, 2 * TOK, KC), BF16),
             vmem((NK, 8 * TOK, KC), BF16),
             vmem((NK, FB, KC), F32),
             vmem((NK, FB, KC), BF16),
             vmem((NK, FB, KC), BF16),
             vmem((NK, FB, KC), BF16),
+            vmem((64, 128), BF16),
+            vmem((64, 128), F32),
             vmem((4, 512, 128), BF16),
             vmem((4, 512, 128), F32),
             vmem((4, 512, 128), BF16),
@@ -368,27 +400,26 @@
             vmem((2, NZ * SHARE, 128), BF16),
             vmem((4, 512, 128), BF16),
             vmem((4, 512, 128), BF16),
-            dma((33,)),
+            dma((34,)),
             dma((14,)), dma((14,)),
             dma((7,)), dma((7,)),
             dma((NK,)), dma((NK,)),
             dma((NK * NX,)), dma((NK * NX,)),
             dma((NK,)), dma((NK,)),
+            dma((NK * NX,)), dma((NK * NX,)),
             dma((NK,)), dma((NK,)),
-            dma((NK * NX * 2,)), dma((NK * NX * 2,)),
-            dma((NK,)), dma((NK,)),
-            dma((3,)), dma((3,)),
+            dma((4,)), dma((4,)),
             dma((NZ,)), dma((NZ,)),
             dma((NZ,)), dma((NZ,)),
             dma((12,)),
         ],
         compiler_params=pltpu.CompilerParams(
-            collective_id=0, has_side_effects=True, vmem_limit_bytes=48 * 1024 * 1024
+            collective_id=0, has_side_effects=True, vmem_limit_bytes=67043328
         ),
         name="window",
     )(
         tokens,
-        norm_gain.reshape(16, FB).astype(F32),
+        norm_gain.reshape(64, 128),
         inner_weight,
         cotangent,
         fragment,
@@ -397,6 +428,14 @@
         lag,
         threshold,
     )
+    return pl.pallas_call(
+        put_out,
+        out_shape=shapes,
+        in_specs=[anywhere] * 3,
+        out_specs=(anywhere,) * 3,
+        scratch_shapes=[vmem(shape.shape, BF16) for shape in shapes] + [dma((6,))],
+        name="put_out",
+    )(*results)
 
 
 def solution(mesh):

time: 115 us -> 92.4 us (0.80)
  Pallas kernels: 105 us -> 89.6 us
  local copies, waits for them, and re-layouts: 8.37 us -> 0 us
    pallas_call x1 -> x2, Pallas kernels: 105 us -> 89.6 us  [the longest x1 87.3 us: shards(): pl.pallas_call(kernel, out_shape=shapes, in_specs=[hbm] * 7 + [smem, smem...]
    unnamed x13 -> x0, local copies, waits for them, and re-layouts: 7.63 us -> none
where the time goes in v2:
time: 92.4 us; the launch traced here: 91.5 us
  Pallas kernels  89.6 us (97%)
  between operations  1.93 us (2%)
    pallas_call x1, Pallas kernels, shards(): pl.pallas_call(kernel, out_shape=shapes, in_specs=[hbm] * 7 + [smem, smem...  87.3 us
    pallas_call x1, Pallas kernels, shards(): pl.pallas_call(put_out, out_shape=shapes, in_specs=[anywhere] * 3, out_sp...  2.23 us

profile of v2, /device:TPU:6, one launch (start us, length us, event | category | flops | bytes accessed | tf_op | source)
XLA Modules:
  0.0 91.5 jit_solution(5321035683256253886)
XLA Ops:
  1.9 87.3 %window.1 = (bf16[1,512,512]{2,1,0:T(8,128)(2,1)}, bf16[1,512,512]{2,1,0:T(8,128)(2,1)}, bf16[512,512]{1,0:T(8,128)(2,1)}) custom-call(bf16[1,128,8192]{2,1,0:T(8,128)(2,1)} %tokens.1, bf16[64,128]{1,0:T(8,128)(2,1)} %bitcast.1, bf16[1,512,512]{2,1,0:T(8,128)(2,1)} %weight.1, bf16[1,128,512]{2,1,0:T(8,128)(2,1)} %cotangent.1, bf16[1,512,512]{2,1,0:T(8,128)(2,1)} %fragment.1, ...), custom_call_target="tpu_custom_call" | custom-call | tf_op jit(solution)/shard_map/window/pallas_call | solution.py:363
  89.3 2.2 %put_out.1 = (bf16[1,512,512]{2,1,0:T(8,128)(2,1)}, bf16[1,512,512]{2,1,0:T(8,128)(2,1)}, bf16[512,512]{1,0:T(8,128)(2,1)}) custom-call(bf16[1,512,512]{2,1,0:T(8,128)(2,1)} %get-tuple-element.6.grad, bf16[1,512,512]{2,1,0:T(8,128)(2,1)} %get-tuple-element.7.mixed, bf16[512,512]{1,0:T(8,128)(2,1)} %get-tuple-element.8.mom), custom_call_target="tpu_custom_call" | custom-call | tf_op jit(solution)/shard_map/put_out/pallas_call | solution.py:431

commit v3 on v2

--- a/solution.py
+++ b/solution.py
@@ -11,14 +11,14 @@
 MU = 0.9
 OUTER_LR = 0.7
 ALPHA = 0.5
-STARTS = (0.0, 4.3, 8.0, 13.0, 19.0)
-STEP = 2.6
+STARTS = (0.0, 5.0, 10.0, 15.0, 23.0)
+STEP = 4.0
 
 NX, NY, NZ = 4, 4, 12
 TOK = 128
 FB = 512
 KV = 512
-NK = 4
+NK = 2
 KC = KV // NK
 SHARE = 96
 PACK = SHARE + 16
@@ -228,8 +228,6 @@
                 sum_z()
             w_copies[1].start()
         if (i, e) == (0, 1):
-            w_copies[2].start()
-            w_copies[3].start()
             cot_copy.start()
 
     rx, ry, ax, gr = {}, {}, {}, {}

time: 92.4 us -> 98.3 us (1.064)
  the two profiles are of different devices: /device:TPU:6 before, /device:TPU:8 now
where the time goes in v3:
time: 98.3 us; the launch traced here: 98.1 us
  Pallas kernels  96.2 us (98%)
  between operations  1.93 us (2%)
    pallas_call x1, Pallas kernels, shards(): pl.pallas_call(kernel, out_shape=shapes, in_specs=[hbm] * 7 + [smem, smem...  94 us
    pallas_call x1, Pallas kernels, shards(): pl.pallas_call(put_out, out_shape=shapes, in_specs=[anywhere] * 3, out_sp...  2.23 us

profile of v3, /device:TPU:8, one launch (start us, length us, event | category | flops | bytes accessed | tf_op | source)
XLA Modules:
  0.0 98.1 jit_solution(14074206652131647476)
XLA Ops:
  1.9 94.0 %window.1 = (bf16[1,512,512]{2,1,0:T(8,128)(2,1)}, bf16[1,512,512]{2,1,0:T(8,128)(2,1)}, bf16[512,512]{1,0:T(8,128)(2,1)}) custom-call(bf16[1,128,8192]{2,1,0:T(8,128)(2,1)} %tokens.1, bf16[64,128]{1,0:T(8,128)(2,1)} %bitcast.1, bf16[1,512,512]{2,1,0:T(8,128)(2,1)} %weight.1, bf16[1,128,512]{2,1,0:T(8,128)(2,1)} %cotangent.1, bf16[1,512,512]{2,1,0:T(8,128)(2,1)} %fragment.1, ...), custom_call_target="tpu_custom_call" | custom-call | tf_op jit(solution)/shard_map/window/pallas_call | solution.py:361
  95.9 2.2 %put_out.1 = (bf16[1,512,512]{2,1,0:T(8,128)(2,1)}, bf16[1,512,512]{2,1,0:T(8,128)(2,1)}, bf16[512,512]{1,0:T(8,128)(2,1)}) custom-call(bf16[1,512,512]{2,1,0:T(8,128)(2,1)} %get-tuple-element.6.grad, bf16[1,512,512]{2,1,0:T(8,128)(2,1)} %get-tuple-element.7.mixed, bf16[512,512]{1,0:T(8,128)(2,1)} %get-tuple-element.8.mom), custom_call_target="tpu_custom_call" | custom-call | tf_op jit(solution)/shard_map/put_out/pallas_call | solution.py:429
